TPU v7x, 32 devices: a whole 2x2x4 slice. The times are simulated.
32 devices in a mesh: lon: 8 (over z, x), lat: 4 (over y, core).
Axes of the slice: x: 2, y: 2, z: 4, core: 2. Of those that a mesh axis runs over, the one named last changes fastest.
Arguments:
- state: float32 [2048, 64, 1024], P('lon', None, 'lat'), may hold values from -6 to 6
Outputs:
- spectrum: float32 [2, 1024, 64, 1024], P(None, 'lon', None, 'lat')
All inputs are finite; a program needn't handle non-finite values.
Results may differ from a plain program's by a relative error of at most 0.00011.
Values sent between devices are 32-bit elements; how exact they have to be, the bound alone decides.
A program may use at most 128 MiB of HBM per device.

v0:
```python
import functools
import math

import jax
import jax.numpy as jnp
import numpy as np
from jax import lax
from jax.experimental import pallas as pl
from jax.experimental.pallas import tpu as pltpu
from jax.sharding import PartitionSpec as P

RADIX = 8
LANES = 128
SUBLANES = 8
TILE = 16


def phase_angle(first_index, second_index, period):
    product = first_index * second_index % period
    return product.astype(jnp.float32) * (2.0 * math.pi / period)


def dense_spectrum(gathered, factor):
    lon_count = gathered.shape[0]
    mode_count = lon_count // 2
    wavenum = lax.broadcasted_iota(jnp.int32, (mode_count, lon_count), 0)
    longitude = lax.broadcasted_iota(jnp.int32, (mode_count, lon_count), 1)
    angles = phase_angle(wavenum, longitude, lon_count)
    real_part = jnp.dot(
        jnp.cos(angles) * factor,
        gathered,
        precision=lax.Precision.HIGHEST,
        preferred_element_type=jnp.float32,
    )
    imag_part = jnp.dot(
        -jnp.sin(angles) * factor,
        gathered,
        precision=lax.Precision.HIGHEST,
        preferred_element_type=jnp.float32,
    )
    return jnp.stack([real_part, imag_part])


def dense_local(state):
    lon_dev, fields, lat_dev = state.shape
    devices = lax.axis_size("lon")
    columns = state.reshape(lon_dev, fields * lat_dev)
    factor = 1.0 / math.sqrt(lon_dev * devices)
    gathered = lax.all_to_all(columns, "lon", split_axis=1, concat_axis=0, tiled=True)
    spectrum = dense_spectrum(gathered, factor)
    shares = lax.all_to_all(spectrum, "lon", split_axis=1, concat_axis=2, tiled=True)
    return shares.reshape(2, shares.shape[1], fields, lat_dev)


def split(value):
    high = value.astype(jnp.bfloat16)
    return high, (value - high.astype(jnp.float32)).astype(jnp.bfloat16)


def build_weights(cos_base, sin_base, cos_turn, sin_turn, w_hi, w_lo):
    modes, points = cos_base.shape

    def put(group, row, column, value):
        high, low = split(value)
        rows, columns = pl.ds(row * modes, modes), pl.ds(column * points, points)
        w_hi[group, rows, columns] = high
        w_lo[group, rows, columns] = low

    def table(residue):
        turn_c = cos_turn[pl.ds(residue, 1), :]
        turn_s = sin_turn[pl.ds(residue, 1), :]
        cos_b, sin_b = cos_base[...], sin_base[...]
        return cos_b * turn_c - sin_b * turn_s, sin_b * turn_c + cos_b * turn_s

    zero = jnp.zeros((modes, points), jnp.float32)
    for group in range(RADIX // 2):
        cos_a, sin_a = table(group)
        if group == 0:
            cos_b, sin_b = table(RADIX // 2)
            entries = ((cos_a, zero), (-sin_a, zero), (zero, cos_b), (zero, -sin_b))
        else:
            cos_b, sin_b = table(RADIX - group)
            entries = ((cos_a, sin_a), (-sin_a, cos_a), (cos_b, -sin_b), (-sin_b, -cos_b))
        for row, pair in enumerate(entries):
            for column, value in enumerate(pair):
                put(group, row, column, value)


def radix_stage(x):
    root = math.sqrt(0.5)
    a, b, c, d = x[0] + x[4], x[0] - x[4], x[2] + x[6], x[2] - x[6]
    e, f, g, h = x[1] + x[5], x[1] - x[5], x[3] + x[7], x[3] - x[7]
    even, odd = a + c, e + g
    diff, total = root * (f - h), root * (f + h)
    return (
        (even + odd, even - odd),
        (b + diff, -d - total),
        (a - c, g - e),
        (b - diff, d - total),
    )


def transform(half, points, grid, packed, w_hi, w_lo, y_hi, y_lo):
    modes = points // 2
    share = modes // RADIX
    block_rows = share * RADIX
    grid_rows = grid.reshape(grid.shape[0] * RADIX * points * SUBLANES, LANES)
    packed_rows = packed.reshape(packed.shape[0] * RADIX * 2 * block_rows * SUBLANES, LANES)

    def field_pair(pair, carry):
        def tile(index, carry):
            first = index * TILE
            for side in range(2):
                x = [
                    grid_rows[
                        pl.ds(
                            ((half * RADIX + d) * points + first) * SUBLANES + 2 * pair + side,
                            TILE,
                            stride=SUBLANES,
                        ),
                        :,
                    ]
                    for d in range(RADIX)
                ]
                for group, values in enumerate(radix_stage(x)):
                    for part, value in enumerate(values):
                        high, low = split(value)
                        rows = pl.ds(pl.multiple_of(part * points + first, TILE), TILE)
                        lanes = pl.ds(side * LANES, LANES)
                        y_hi[group, rows, lanes] = high
                        y_lo[group, rows, lanes] = low
            return carry

        lax.fori_loop(0, points // TILE, tile, 0)

        def residues(group, carry):
            dot = functools.partial(jnp.dot, preferred_element_type=jnp.float32)
            high = y_hi[group]
            out = dot(w_hi[group], high) + dot(w_hi[group], y_lo[group]) + dot(w_lo[group], high)
            other = jnp.where(group == 0, RADIX // 2, RADIX - group)
            for which, residue in enumerate((group, other)):
                for part in range(2):
                    row = (2 * which + part) * modes
                    for e in range(RADIX):
                        for side in range(2):
                            base = ((half * RADIX + e) * 2 + part) * block_rows
                            packed_rows[
                                pl.ds(
                                    (base + residue) * SUBLANES + 2 * pair + side,
                                    share,
                                    stride=RADIX * SUBLANES,
                                ),
                                :,
                            ] = out[
                                row + e * share : row + (e + 1) * share,
                                side * LANES : (side + 1) * LANES,
                            ]
            return carry

        lax.fori_loop(0, RADIX // 2, residues, 0)
        return carry

    lax.fori_loop(0, SUBLANES // 2, field_pair, 0)


def kernel(
    halves,
    state, cos_base, sin_base, cos_turn, sin_turn, out,
    grid, packed, w_hi, w_lo, y_hi, y_lo,
    send_sem, recv_sem, own_sem,
):
    points = state.shape[0]
    me = lax.axis_index("lon")
    ring, side = me // 2, lax.rem(me, 2)

    def peer(dz, dx):
        return lax.rem(ring + dz + 4, 4) * 2 + lax.rem(side + dx, 2)

    offsets = [(2, 1), (2, 0), (1, 1), (1, 0), (3, 1), (3, 0), (0, 1)]

    def fields(owner):
        return pl.ds(pl.multiple_of(owner * SUBLANES, SUBLANES), SUBLANES)

    def lanes(half):
        return pl.ds(half * LANES, LANES)

    def source(phase, half, target):
        if phase == 0:
            return state.at[:, fields(target), lanes(half)]
        return packed.at[half, target]

    def landing(phase, half, origin):
        if phase == 0:
            return grid.at[half, origin]
        return out.at[:, :, fields(origin), lanes(half)]

    def direct(phase, half, index):
        target = peer(*offsets[index])
        return pltpu.make_async_remote_copy(
            src_ref=source(phase, half, target),
            dst_ref=landing(phase, half, me),
            send_sem=send_sem.at[phase, half, index],
            recv_sem=recv_sem.at[phase, half, index],
            device_id={"lon": target},
            device_id_type=pl.DeviceIdType.MESH,
        )

    def own(phase, half):
        return pltpu.make_async_copy(
            source(phase, half, me), landing(phase, half, me), own_sem.at[phase, half]
        )

    def send(phase, half):
        for index in range(len(offsets)):
            direct(phase, half, index).start()
        own(phase, half).start()

    def receive(phase, half):
        own(phase, half).wait()
        for index, (dz, dx) in enumerate(offsets):
            origin = peer(-dz, dx)
            pltpu.make_async_remote_copy(
                src_ref=landing(phase, half, origin),
                dst_ref=landing(phase, half, origin),
                send_sem=send_sem.at[phase, half, index],
                recv_sem=recv_sem.at[phase, half, index],
                device_id={"lon": origin},
                device_id_type=pl.DeviceIdType.MESH,
            ).wait_recv()

    barrier = pltpu.get_barrier_semaphore()
    for dz, dx in offsets:
        pl.semaphore_signal(
            barrier, inc=1, device_id={"lon": peer(dz, dx)}, device_id_type=pl.DeviceIdType.MESH
        )
    pl.semaphore_wait(barrier, len(offsets))

    for half in range(halves):
        send(0, half)
    build_weights(cos_base, sin_base, cos_turn, sin_turn, w_hi, w_lo)
    for half in range(halves):
        receive(0, half)
        transform(half, points, grid, packed, w_hi, w_lo, y_hi, y_lo)
        send(1, half)
    for half in range(halves):
        receive(1, half)
    for phase in range(2):
        for half in range(halves):
            for index in range(len(offsets)):
                direct(phase, half, index).wait_send()


def angle_tables(points):
    count = points * RADIX
    scale = 1.0 / math.sqrt(count)
    place = np.arange(points)
    base = 2.0 * np.pi / count * (RADIX * np.arange(points // 2)[:, None] * place % count)
    turn = 2.0 * np.pi / count * (np.arange(RADIX)[:, None] * place % count)
    tables = (scale * np.cos(base), scale * np.sin(base), np.cos(turn), np.sin(turn))
    return [jnp.asarray(table.astype(np.float32)) for table in tables]


def fused_local(state):
    points, fields, lat_dev = state.shape
    halves = lat_dev // LANES
    modes = points // 2
    vmem = pl.BlockSpec(memory_space=pltpu.VMEM)
    hbm = pl.BlockSpec(memory_space=pl.ANY)
    half_shape = (2, modes, SUBLANES, LANES)
    return pl.pallas_call(
        functools.partial(kernel, halves),
        out_shape=pltpu.VMEM((2, modes, fields, lat_dev), jnp.float32),
        in_specs=[hbm] + [vmem] * 4,
        out_specs=hbm,
        scratch_shapes=[
            pltpu.VMEM((halves, RADIX, points, SUBLANES, LANES), jnp.float32),
            pltpu.VMEM((halves, RADIX) + half_shape, jnp.float32),
            pltpu.VMEM((RADIX // 2, 4 * modes, 2 * points), jnp.bfloat16),
            pltpu.VMEM((RADIX // 2, 4 * modes, 2 * points), jnp.bfloat16),
            pltpu.VMEM((RADIX // 2, 2 * points, 2 * LANES), jnp.bfloat16),
            pltpu.VMEM((RADIX // 2, 2 * points, 2 * LANES), jnp.bfloat16),
            pltpu.SemaphoreType.DMA((2, halves, RADIX - 1)),
            pltpu.SemaphoreType.DMA((2, halves, RADIX - 1)),
            pltpu.SemaphoreType.DMA((2, halves)),
        ],
        compiler_params=pltpu.CompilerParams(
            collective_id=0, has_side_effects=True, vmem_limit_bytes=41 * 1024 * 1024
        ),
    )(state, *angle_tables(points))


def solution(mesh):
    devices = mesh.shape["lon"]

    def local(state):
        points, fields, lat_dev = state.shape
        fits = (
            devices == RADIX
            and fields == RADIX * SUBLANES
            and points == 2 * LANES
            and lat_dev == 2 * LANES
        )
        return fused_local(state) if fits else dense_local(state)

    return jax.shard_map(
        local,
        mesh=mesh,
        in_specs=(P("lon", None, "lat"),),
        out_specs=P(None, "lon", None, "lat"),
        check_vma=False,
    )
```

profile of v0, /device:TPU:13, one launch (start us, length us, event | category | flops | bytes accessed | tf_op | source)
XLA Modules:
  0.0 731.8 jit_solution(13366672594763235732)
XLA Ops:
  0.0 725.7 %shard_map.55 = f32[2,128,64,256]{3,2,1,0:T(8,128)S(1)} custom-call(f32[256,64,256]{2,1,0:T(8,128)} %state.1, f32[128,256]{1,0:T(8,128)} %constant.8.clone.cos_base, f32[128,256]{1,0:T(8,128)} %constant.9.clone.sin_base, f32[8,256]{1,0:T(8,128)} %constant.10.clone.cos_turn, f32[8,256]{1,0:T(8,128)} %constant.11.clone.sin_turn), custom_call_target="tpu_custom_call" | custom-call | tf_op jit(solution)/shard_map/pallas_call | solution.py:270
  725.7 6.2 copy.7
where the time goes:
time: 732 us
  Pallas kernels  726 us (99%)
    pallas_call x1, Pallas kernels, fused_local(): pl.pallas_call(functools.partial(kernel, halves), out_shape=pltpu.VMEM((2...  726 us

commit v1 on v0

v1 whole, which is shorter than its diff:
```python
import functools
import math

import jax
import jax.numpy as jnp
import numpy as np
from jax import lax
from jax.experimental import pallas as pl
from jax.experimental.pallas import tpu as pltpu
from jax.sharding import PartitionSpec as P

RADIX = 8
LANES = 128
SUBLANES = 8
TILE = 16
SIDE = RADIX // 2
PAIRS = SUBLANES // 2
EXTRA = 24
LAG = 5
GRID_SLOTS = 7
OTHER_SLOTS = 3
CODED_SLOTS = 3
ARRIVED_SLOTS = 4
DONE_SLOTS = 7
CROSS_SLOTS = 4
VMEM_LIMIT = 46 * 1024 * 1024


def phase_angle(first_index, second_index, period):
    product = first_index * second_index % period
    return product.astype(jnp.float32) * (2.0 * math.pi / period)


def dense_spectrum(gathered, factor):
    lon_count = gathered.shape[0]
    mode_count = lon_count // 2
    wavenum = lax.broadcasted_iota(jnp.int32, (mode_count, lon_count), 0)
    longitude = lax.broadcasted_iota(jnp.int32, (mode_count, lon_count), 1)
    angles = phase_angle(wavenum, longitude, lon_count)
    real_part = jnp.dot(
        jnp.cos(angles) * factor,
        gathered,
        precision=lax.Precision.HIGHEST,
        preferred_element_type=jnp.float32,
    )
    imag_part = jnp.dot(
        -jnp.sin(angles) * factor,
        gathered,
        precision=lax.Precision.HIGHEST,
        preferred_element_type=jnp.float32,
    )
    return jnp.stack([real_part, imag_part])


def dense_local(state):
    lon_dev, fields, lat_dev = state.shape
    devices = lax.axis_size("lon")
    columns = state.reshape(lon_dev, fields * lat_dev)
    factor = 1.0 / math.sqrt(lon_dev * devices)
    gathered = lax.all_to_all(columns, "lon", split_axis=1, concat_axis=0, tiled=True)
    spectrum = dense_spectrum(gathered, factor)
    shares = lax.all_to_all(spectrum, "lon", split_axis=1, concat_axis=2, tiled=True)
    return shares.reshape(2, shares.shape[1], fields, lat_dev)


def split(value):
    high = value.astype(jnp.bfloat16)
    return high, (value - high.astype(jnp.float32)).astype(jnp.bfloat16)


def split_table(table):
    high = table.astype(jnp.bfloat16)
    return high, (table - high.astype(np.float64)).astype(jnp.bfloat16)


def dft_rows(wavenums, places, count):
    angle = 2.0 * np.pi / count * (wavenums[:, None] * places[None] % count)
    scale = 1.0 / math.sqrt(count)
    return scale * np.cos(angle), -scale * np.sin(angle)


def by_owner(parts):
    shaped = [part.reshape(SIDE, -1, part.shape[1]) for part in parts]
    return np.stack(shaped, 1).reshape(-1, parts[0].shape[1])


def side_tables(points, side):
    count, band = RADIX * points, RADIX * points // 4
    places = side * (count // 2) + np.arange(count // 2)
    step = 2 * np.arange(band // 2)

    def rows(first):
        return by_owner(dft_rows(first + step, places, count))

    own = [rows(side * band + parity).reshape(SIDE, 1, -1, count // 2) for parity in range(2)]
    own = np.concatenate(own, 1).reshape(2 * band, count // 2)
    even, odd = rows((1 - side) * band), rows((1 - side) * band + 1)
    power = (even * even).sum(1)
    spread = (odd @ even.T) * np.where(power > 1e-9, 1.0 / np.maximum(power, 1e-9), 0.0)
    left = odd - spread @ even
    picked, columns = [], []
    for _ in range(EXTRA):
        row, column = np.unravel_index(np.argmax(np.abs(left)), left.shape)
        picked.append(row)
        columns.append(left[:, column] / left[row, column])
        left = left - np.outer(columns[-1], left[row])
    columns = np.stack(columns, 1)
    mix = np.linalg.solve(columns[picked].T, columns.T).T
    rank, padded = band + EXTRA, -(-(band + EXTRA) // 16) * 16
    sent = np.zeros((padded, count // 2))
    sent[:rank] = np.concatenate([even, odd[picked]])
    fill = np.zeros((band, padded))
    fill[:, :rank] = np.concatenate([spread - mix @ spread[picked], mix], 1)
    return own, sent, fill


def all_tables(points):
    sides = [side_tables(points, side) for side in range(2)]
    out = []
    for tables in zip(*sides):
        for piece in split_table(np.stack(tables)):
            out.append(jnp.asarray(piece))
    return out


def kernel(
    chunks, rank,
    state, own_hi_all, own_lo_all, sent_hi_all, sent_lo_all, fill_hi_all, fill_lo_all, out,
    inb, grid, other, coded, arrived, done, cross,
    own_hi, own_lo, sent_hi, sent_lo, fill_hi, fill_lo, x_hi, x_lo, c_hi, c_lo,
    in_sem, table_sem, xs_send, xs_recv, zs_send, zs_recv, m_send, m_recv,
    zo_send, zo_recv, xo_send, xo_recv,
):
    points = state.shape[0]
    modes = points // 2
    groups = chunks // PAIRS
    padded = coded.shape[1]
    me = lax.axis_index("lon")
    z, x = me // 2, lax.rem(me, 2)
    row, side = lax.rem(z, 2), z // 2
    place = lax.rem(me, SIDE)
    beside = place + 1 - 2 * x
    inner = lax.rem((z + 1) // 2, 2) == 1
    outer = lax.rem((z + 1) // 2, 2) == 0
    x_peer = me + 1 - 2 * x
    z_peer = me + 2 - 4 * row
    m_peer = (3 - z) * 2 + x

    def remote(source, target, send, recv, peer):
        return pltpu.make_async_remote_copy(
            src_ref=source, dst_ref=target, send_sem=send, recv_sem=recv,
            device_id={"lon": peer}, device_id_type=pl.DeviceIdType.MESH,
        )

    def load(group, half):
        slot = lax.rem(group, 2)
        fields = pl.ds(pl.multiple_of(group * SUBLANES, SUBLANES), SUBLANES)
        return pltpu.make_async_copy(
            state.at[:, fields, half * LANES : (half + 1) * LANES],
            inb.at[slot, half], in_sem.at[slot, half],
        )

    def samples_x(t, target_place):
        slot = lax.rem(t, GRID_SLOTS)
        return remote(
            other.at[lax.rem(t, OTHER_SLOTS)], grid.at[slot, target_place],
            xs_send.at[lax.rem(t, OTHER_SLOTS)], xs_recv.at[slot], x_peer,
        )

    def samples_z(t, which, line):
        slot = lax.rem(t, GRID_SLOTS)
        ref = grid.at[slot, line * 2 + which]
        return remote(ref, ref, zs_send.at[slot, which], zs_recv.at[slot, which], z_peer)

    def code(t):
        rows = pl.ds(0, rank)
        here, there = lax.rem(t, CODED_SLOTS), lax.rem(t, ARRIVED_SLOTS)
        return remote(
            coded.at[here, rows], arrived.at[there, rows], m_send.at[here], m_recv.at[there], m_peer
        )

    def modes_z(t, which, line):
        slot = lax.rem(t, DONE_SLOTS)
        ref = done.at[slot, line * 2 + which]
        return remote(ref, ref, zo_send.at[slot, which], zo_recv.at[slot, which], z_peer)

    def modes_x(t):
        slot, there = lax.rem(t, DONE_SLOTS), lax.rem(t, CROSS_SLOTS)
        return remote(
            done.at[slot, beside], cross.at[there], xo_send.at[slot], xo_recv.at[there], x_peer
        )

    tables = [
        pltpu.make_async_copy(source.at[which], target, table_sem.at[index])
        for index, (source, which, target) in enumerate((
            (sent_hi_all, side, sent_hi), (sent_lo_all, side, sent_lo),
            (own_hi_all, side, own_hi), (own_lo_all, side, own_lo),
            (fill_hi_all, 1 - side, fill_hi), (fill_lo_all, 1 - side, fill_lo),
        ))
    ]
    in_rows = inb.reshape(2 * 2 * points * SUBLANES, LANES)
    out_rows = out.reshape(2 * modes * groups * 2 * SUBLANES, LANES)
    k_rows = groups * 2 * SUBLANES

    def arrange(t):
        group, pair = t // PAIRS, lax.rem(t, PAIRS)

        @pl.when(pair == 0)
        def _():
            for half in range(2):
                load(group, half).wait()

        @pl.when(t >= OTHER_SLOTS)
        def _():
            samples_x(t - OTHER_SLOTS, place).wait_send()

        slot, spare = lax.rem(t, GRID_SLOTS), lax.rem(t, OTHER_SLOTS)

        def tile(index, carry):
            first = pl.multiple_of(index * TILE, TILE)
            for field in range(2):
                lanes = pl.ds(field * LANES, LANES)

                def read(half):
                    base = ((lax.rem(group, 2) * 2 + half) * points + first) * SUBLANES
                    return in_rows[pl.ds(base + 2 * pair + field, TILE, stride=SUBLANES), :]

                other[spare, pl.ds(first, TILE), lanes] = read(1 - x)
                grid[slot, place, pl.ds(first, TILE), lanes] = read(x)
            return carry

        lax.fori_loop(0, points // TILE, tile, 0)

        @pl.when((pair == PAIRS - 1) & (group + 2 < groups))
        def _():
            for half in range(2):
                load(group + 2, half).start()

        samples_x(t, place).start()

    def store(t, half, ref):
        group, pair = t // PAIRS, lax.rem(t, PAIRS)
        share = modes // 2
        for parity in range(2):
            for part in range(2):
                for field in range(2):
                    first = (part * modes + parity) * k_rows
                    base = first + (group * 2 + half) * SUBLANES + 2 * pair + field
                    out_rows[pl.ds(base, share, stride=2 * k_rows), :] = ref[
                        pl.ds((parity * 2 + part) * share, share), pl.ds(field * LANES, LANES)
                    ]

    def dot3(a_hi, a_lo, b_hi, b_lo):
        dot = functools.partial(jnp.dot, preferred_element_type=jnp.float32)
        return dot(a_hi, b_hi) + dot(a_hi, b_lo) + dot(a_lo, b_hi)

    def encode(t):
        slot, here = lax.rem(t, GRID_SLOTS), lax.rem(t, CODED_SLOTS)
        for which in range(SIDE):

            def tile(index, carry):
                first = pl.multiple_of(index * 32, 32)
                high, low = split(grid[slot, which, pl.ds(first, 32), :])
                rows = pl.ds(pl.multiple_of(which * points + first, 32), 32)
                x_hi[rows, :] = high
                x_lo[rows, :] = low
                return carry

            lax.fori_loop(0, points // 32, tile, 0)

        @pl.when(t >= CODED_SLOTS)
        def _():
            code(t - CODED_SLOTS).wait_send()

        coded[here] = dot3(sent_hi[...], sent_lo[...], x_hi[...], x_lo[...])
        code(t).start()

    def own_modes(t):
        slot = lax.rem(t, DONE_SLOTS)

        @pl.when(t >= DONE_SLOTS)
        def _():
            for which in range(2):
                modes_z(t - DONE_SLOTS, which, 1 - row).wait_send()
            modes_x(t - DONE_SLOTS).wait_send()

        def block(which, carry):
            rows = pl.ds(pl.multiple_of(which * points, points), points)
            done[slot, which] = dot3(own_hi[rows, :], own_lo[rows, :], x_hi[...], x_lo[...])
            return carry

        lax.fori_loop(0, SIDE, block, 0)

    def decode(t):
        slot, there = lax.rem(t, DONE_SLOTS), lax.rem(t, ARRIVED_SLOTS)

        def tile(index, carry):
            rows = pl.ds(pl.multiple_of(index * 32, 32), 32)
            high, low = split(arrived[there, rows, :])
            c_hi[rows, :] = high
            c_lo[rows, :] = low
            return carry

        lax.fori_loop(0, padded // 32, tile, 0)
        odd = dot3(fill_hi[...], fill_lo[...], c_hi[...], c_lo[...])
        share = modes
        for which in range(SIDE):
            rows = slice(which * share, (which + 1) * share)
            done[slot, which, :share] += arrived[there, rows]
            done[slot, which, share:] += odd[rows]

    for group in range(2):
        for half in range(2):
            load(group, half).start()

    @pl.when(inner)
    def _():
        for copy in tables:
            copy.start()

    arrived[:, rank:padded] = jnp.zeros((arrived.shape[0], padded - rank, arrived.shape[2]), jnp.float32)
    barrier = pltpu.get_barrier_semaphore()
    for peer in (x_peer, z_peer, m_peer):
        pl.semaphore_signal(
            barrier, inc=1, device_id={"lon": peer}, device_id_type=pl.DeviceIdType.MESH
        )
    pl.semaphore_wait(barrier, 3)

    arrange(0)

    @pl.when(outer)
    def _():
        samples_z(0, x, row).start()

    def step(i, carry):
        @pl.when(outer & (i >= 2) & (i < chunks + 2))
        def _():
            for which in range(2):
                samples_z(i - 2, which, row).wait_send()

        @pl.when(i + 1 < chunks)
        def _():
            arrange(i + 1)

        @pl.when(i < chunks)
        def _():
            samples_x(i, beside).wait_recv()

        @pl.when(outer & (i < chunks))
        def _():
            samples_z(i, 1 - x, row).start()

            @pl.when(i + 1 < chunks)
            def _():
                samples_z(i + 1, x, row).start()

        @pl.when(outer & (i >= LAG) & (i < chunks + LAG))
        def _():
            t = i - LAG
            modes_z(t, 1 - x, row).wait_recv()
            modes_x(t).start()
            modes_z(t, x, row).wait_recv()
            store(t, x, done.at[lax.rem(t, DONE_SLOTS), place])

        @pl.when(outer & (i >= LAG + 1) & (i < chunks + LAG + 1))
        def _():
            t = i - LAG - 1
            modes_x(t).wait_send()
            modes_x(t).wait_recv()
            store(t, 1 - x, cross.at[lax.rem(t, CROSS_SLOTS)])

        @pl.when(inner & (i < chunks))
        def _():
            for which in range(2):
                samples_z(i, which, 1 - row).wait_recv()

            @pl.when(i == 0)
            def _():
                for copy in tables:
                    copy.wait()

            encode(i)
            own_modes(i)

        @pl.when(inner & (i >= 1) & (i < chunks + 1))
        def _():
            t = i - 1
            code(t).wait_recv()
            decode(t)
            modes_z(t, 1 - x, 1 - row).start()
            modes_x(t).start()
            modes_z(t, x, 1 - row).start()
            store(t, x, done.at[lax.rem(t, DONE_SLOTS), place])

        @pl.when(inner & (i >= 2) & (i < chunks + 2))
        def _():
            t = i - 2
            modes_x(t).wait_recv()
            store(t, 1 - x, cross.at[lax.rem(t, CROSS_SLOTS)])

        return carry

    lax.fori_loop(0, chunks + LAG + 1, step, 0)

    for back in range(OTHER_SLOTS):
        samples_x(chunks - 1 - back, place).wait_send()

    @pl.when(inner)
    def _():
        for back in range(CODED_SLOTS):
            code(chunks - 1 - back).wait_send()
        for back in range(DONE_SLOTS):
            for which in range(2):
                modes_z(chunks - 1 - back, which, 1 - row).wait_send()
            modes_x(chunks - 1 - back).wait_send()


def fused_local(state):
    points, fields, lat_dev = state.shape
    modes = points // 2
    groups = fields // SUBLANES
    chunks = groups * PAIRS
    tables = all_tables(points)
    padded = tables[2].shape[1]
    rank = RADIX * points // 4 + EXTRA
    vmem = pl.BlockSpec(memory_space=pltpu.VMEM)
    hbm = pl.BlockSpec(memory_space=pl.ANY)
    wide = 2 * LANES
    dma = pltpu.SemaphoreType.DMA

    def f32(*shape):
        return pltpu.VMEM(shape, jnp.float32)

    def bf16(*shape):
        return pltpu.VMEM(shape, jnp.bfloat16)

    result = pl.pallas_call(
        functools.partial(kernel, chunks, rank),
        out_shape=pltpu.VMEM((2, modes, groups, 2, SUBLANES, LANES), jnp.float32),
        in_specs=[hbm] * (1 + len(tables)),
        out_specs=vmem,
        scratch_shapes=[
            f32(2, 2, points, SUBLANES, LANES),
            f32(GRID_SLOTS, SIDE, points, wide),
            f32(OTHER_SLOTS, points, wide),
            f32(CODED_SLOTS, padded, wide),
            f32(ARRIVED_SLOTS, padded, wide),
            f32(DONE_SLOTS, SIDE, points, wide),
            f32(CROSS_SLOTS, points, wide),
            *[bf16(*table.shape[1:]) for table in tables],
            bf16(SIDE * points, wide),
            bf16(SIDE * points, wide),
            bf16(padded, wide),
            bf16(padded, wide),
            dma((2, 2)),
            dma((len(tables),)),
            dma((OTHER_SLOTS,)),
            dma((GRID_SLOTS,)),
            dma((GRID_SLOTS, 2)),
            dma((GRID_SLOTS, 2)),
            dma((CODED_SLOTS,)),
            dma((ARRIVED_SLOTS,)),
            dma((DONE_SLOTS, 2)),
            dma((DONE_SLOTS, 2)),
            dma((DONE_SLOTS,)),
            dma((CROSS_SLOTS,)),
        ],
        compiler_params=pltpu.CompilerParams(
            collective_id=0, has_side_effects=True, vmem_limit_bytes=VMEM_LIMIT
        ),
    )(state, *tables)
    return result.transpose(0, 1, 2, 4, 3, 5).reshape(2, modes, fields, lat_dev)


def solution(mesh):
    devices = mesh.shape["lon"]

    def local(state):
        points, fields, lat_dev = state.shape
        fits = (
            devices == RADIX
            and fields == RADIX * SUBLANES
            and points == 2 * LANES
            and lat_dev == 2 * LANES
        )
        return fused_local(state) if fits else dense_local(state)

    return jax.shard_map(
        local,
        mesh=mesh,
        in_specs=(P("lon", None, "lat"),),
        out_specs=P(None, "lon", None, "lat"),
        check_vma=False,
    )
```

time: 732 us -> 418 us (0.57)
  the two profiles are of different devices: /device:TPU:13 before, /device:TPU:0 now
where the time goes in v1:
time: 418 us
  Pallas kernels  412 us (99%)
  local copies, waits for them, and re-layouts  6.16 us (1%)
    pallas_call x1, Pallas kernels, fused_local(): pl.pallas_call(functools.partial(kernel, chunks, rank), out_shape=pltpu.V...  412 us

profile of v1, /device:TPU:0, one launch (start us, length us, event | category | flops | bytes accessed | tf_op | source)
XLA Modules:
  0.0 417.8 jit_solution(12435002770710543898)
XLA Ops:
  0.0 411.6 %shard_map.73 = f32[2,128,8,2,8,128]{5,4,3,2,1,0:T(8,128)S(1)} custom-call(f32[256,64,256]{2,1,0:T(8,128)} %state.1, bf16[2,1024,1024]{2,1,0:T(8,128)(2,1)} %constant.12.clone.own_hi_all, bf16[2,1024,1024]{2,1,0:T(8,128)(2,1)} %constant.13.clone.own_lo_all, bf16[2,544,1024]{2,1,0:T(8,128)(2,1)} %constant.14.clone.sent_hi_all, ...), custom_call_target="tpu_custom_call" | custom-call | tf_op jit(solution)/shard_map/pallas_call | solution.py:437
  411.6 6.2 %copy.9 = f32[2,128,64,256]{3,2,1,0:T(8,128)} copy(f32[2,128,64,256]{3,2,1,0:T(8,128)S(1)} %bitcast.3) | data formatting | bytes 33554432

commit v2 on v1

--- a/solution.py
+++ b/solution.py
@@ -14,15 +14,18 @@
 SUBLANES = 8
 TILE = 16
 SIDE = RADIX // 2
-PAIRS = SUBLANES // 2
+FIELDS = 1
+PIECES = SUBLANES // FIELDS
+AHEAD = 2
+SENT_LAG = 2
 EXTRA = 24
-LAG = 5
-GRID_SLOTS = 7
-OTHER_SLOTS = 3
+LAG = 7
+GRID_SLOTS = 9
+OTHER_SLOTS = 4
 CODED_SLOTS = 3
 ARRIVED_SLOTS = 4
-DONE_SLOTS = 7
-CROSS_SLOTS = 4
+DONE_SLOTS = 9
+CROSS_SLOTS = 5
 VMEM_LIMIT = 46 * 1024 * 1024
 
 
@@ -108,9 +111,10 @@
     mix = np.linalg.solve(columns[picked].T, columns.T).T
     rank, padded = band + EXTRA, -(-(band + EXTRA) // 16) * 16
     sent = np.zeros((padded, count // 2))
-    sent[:rank] = np.concatenate([even, odd[picked]])
+    sent[:rank] = np.concatenate([even[: band // 2], odd[picked], even[band // 2 :]])
     fill = np.zeros((band, padded))
-    fill[:, :rank] = np.concatenate([spread - mix @ spread[picked], mix], 1)
+    spread = spread - mix @ spread[picked]
+    fill[:, :rank] = np.concatenate([spread[:, : band // 2], mix, spread[:, band // 2 :]], 1)
     return own, sent, fill
 
 
@@ -133,8 +137,8 @@
 ):
     points = state.shape[0]
     modes = points // 2
-    groups = chunks // PAIRS
-    padded = coded.shape[1]
+    groups = chunks // PIECES
+    padded, band = coded.shape[1], rank - EXTRA
     me = lax.axis_index("lon")
     z, x = me // 2, lax.rem(me, 2)
     row, side = lax.rem(z, 2), z // 2
@@ -160,34 +164,45 @@
             inb.at[slot, half], in_sem.at[slot, half],
         )
 
-    def samples_x(t, target_place):
+    def cut(part):
+        return pl.ds(part * modes, modes)
+
+    def samples_x(t, target_place, part):
+        here, slot = lax.rem(t, OTHER_SLOTS), lax.rem(t, GRID_SLOTS)
+        return remote(
+            other.at[here, cut(part)], grid.at[slot, target_place, cut(part)],
+            xs_send.at[here, part], xs_recv.at[slot, part], x_peer,
+        )
+
+    def samples_z(t, which, line, part):
         slot = lax.rem(t, GRID_SLOTS)
-        return remote(
-            other.at[lax.rem(t, OTHER_SLOTS)], grid.at[slot, target_place],
-            xs_send.at[lax.rem(t, OTHER_SLOTS)], xs_recv.at[slot], x_peer,
-        )
-
-    def samples_z(t, which, line):
-        slot = lax.rem(t, GRID_SLOTS)
-        ref = grid.at[slot, line * 2 + which]
-        return remote(ref, ref, zs_send.at[slot, which], zs_recv.at[slot, which], z_peer)
-
-    def code(t):
-        rows = pl.ds(0, rank)
+        ref = grid.at[slot, line * 2 + which, cut(part)]
+        return remote(ref, ref, zs_send.at[slot, which, part], zs_recv.at[slot, which, part], z_peer)
+
+    def evens(line):
+        return line * (band // 2 + EXTRA)
+
+    def code(t, part, line):
+        if part == 0:
+            rows = pl.ds(evens(line), band // 2)
+        else:
+            rows = pl.ds((1 - line) * (band // 2), band // 2 + EXTRA)
         here, there = lax.rem(t, CODED_SLOTS), lax.rem(t, ARRIVED_SLOTS)
         return remote(
-            coded.at[here, rows], arrived.at[there, rows], m_send.at[here], m_recv.at[there], m_peer
-        )
-
-    def modes_z(t, which, line):
+            coded.at[here, rows], arrived.at[there, rows],
+            m_send.at[here, part], m_recv.at[there, part], m_peer,
+        )
+
+    def modes_z(t, which, line, part):
         slot = lax.rem(t, DONE_SLOTS)
-        ref = done.at[slot, line * 2 + which]
-        return remote(ref, ref, zo_send.at[slot, which], zo_recv.at[slot, which], z_peer)
-
-    def modes_x(t):
+        ref = done.at[slot, line * 2 + which, cut(part)]
+        return remote(ref, ref, zo_send.at[slot, which, part], zo_recv.at[slot, which, part], z_peer)
+
+    def modes_x(t, part):
         slot, there = lax.rem(t, DONE_SLOTS), lax.rem(t, CROSS_SLOTS)
         return remote(
-            done.at[slot, beside], cross.at[there], xo_send.at[slot], xo_recv.at[there], x_peer
+            done.at[slot, beside, cut(part)], cross.at[there, cut(part)],
+            xo_send.at[slot, part], xo_recv.at[there, part], x_peer,
         )
 
     tables = [
@@ -203,27 +218,28 @@
     k_rows = groups * 2 * SUBLANES
 
     def arrange(t):
-        group, pair = t // PAIRS, lax.rem(t, PAIRS)
-
-        @pl.when(pair == 0)
+        group, piece = t // PIECES, lax.rem(t, PIECES)
+
+        @pl.when(piece == 0)
         def _():
             for half in range(2):
                 load(group, half).wait()
 
         @pl.when(t >= OTHER_SLOTS)
         def _():
-            samples_x(t - OTHER_SLOTS, place).wait_send()
+            for part in range(2):
+                samples_x(t - OTHER_SLOTS, place, part).wait_send()
 
         slot, spare = lax.rem(t, GRID_SLOTS), lax.rem(t, OTHER_SLOTS)
 
         def tile(index, carry):
             first = pl.multiple_of(index * TILE, TILE)
-            for field in range(2):
+            for field in range(FIELDS):
                 lanes = pl.ds(field * LANES, LANES)
 
                 def read(half):
                     base = ((lax.rem(group, 2) * 2 + half) * points + first) * SUBLANES
-                    return in_rows[pl.ds(base + 2 * pair + field, TILE, stride=SUBLANES), :]
+                    return in_rows[pl.ds(base + FIELDS * piece + field, TILE, stride=SUBLANES), :]
 
                 other[spare, pl.ds(first, TILE), lanes] = read(1 - x)
                 grid[slot, place, pl.ds(first, TILE), lanes] = read(x)
@@ -231,21 +247,19 @@
 
         lax.fori_loop(0, points // TILE, tile, 0)
 
-        @pl.when((pair == PAIRS - 1) & (group + 2 < groups))
+        @pl.when((piece == PIECES - 1) & (group + 2 < groups))
         def _():
             for half in range(2):
                 load(group + 2, half).start()
 
-        samples_x(t, place).start()
-
     def store(t, half, ref):
-        group, pair = t // PAIRS, lax.rem(t, PAIRS)
+        group, piece = t // PIECES, lax.rem(t, PIECES)
         share = modes // 2
         for parity in range(2):
             for part in range(2):
-                for field in range(2):
+                for field in range(FIELDS):
                     first = (part * modes + parity) * k_rows
-                    base = first + (group * 2 + half) * SUBLANES + 2 * pair + field
+                    base = first + (group * 2 + half) * SUBLANES + FIELDS * piece + field
                     out_rows[pl.ds(base, share, stride=2 * k_rows), :] = ref[
                         pl.ds((parity * 2 + part) * share, share), pl.ds(field * LANES, LANES)
                     ]
@@ -270,19 +284,22 @@
 
         @pl.when(t >= CODED_SLOTS)
         def _():
-            code(t - CODED_SLOTS).wait_send()
+            for part in range(2):
+                code(t - CODED_SLOTS, part, row).wait_send()
 
         coded[here] = dot3(sent_hi[...], sent_lo[...], x_hi[...], x_lo[...])
-        code(t).start()
+        for part in range(2):
+            code(t, part, row).start()
 
     def own_modes(t):
         slot = lax.rem(t, DONE_SLOTS)
 
         @pl.when(t >= DONE_SLOTS)
         def _():
-            for which in range(2):
-                modes_z(t - DONE_SLOTS, which, 1 - row).wait_send()
-            modes_x(t - DONE_SLOTS).wait_send()
+            for part in range(2):
+                for which in range(2):
+                    modes_z(t - DONE_SLOTS, which, 1 - row, part).wait_send()
+                modes_x(t - DONE_SLOTS, part).wait_send()
 
         def block(which, carry):
             rows = pl.ds(pl.multiple_of(which * points, points), points)
@@ -290,6 +307,12 @@
             return carry
 
         lax.fori_loop(0, SIDE, block, 0)
+
+    def add_evens(t, line):
+        slot, there = lax.rem(t, DONE_SLOTS), lax.rem(t, ARRIVED_SLOTS)
+        for which in range(2):
+            first = pl.multiple_of(evens(line) + which * modes, SUBLANES)
+            done[slot, line * 2 + which, :modes] += arrived[there, pl.ds(first, modes), :]
 
     def decode(t):
         slot, there = lax.rem(t, DONE_SLOTS), lax.rem(t, ARRIVED_SLOTS)
@@ -303,76 +326,104 @@
 
         lax.fori_loop(0, padded // 32, tile, 0)
         odd = dot3(fill_hi[...], fill_lo[...], c_hi[...], c_lo[...])
-        share = modes
         for which in range(SIDE):
-            rows = slice(which * share, (which + 1) * share)
-            done[slot, which, :share] += arrived[there, rows]
-            done[slot, which, share:] += odd[rows]
-
-    for group in range(2):
-        for half in range(2):
-            load(group, half).start()
+            done[slot, which, modes:] += odd[which * modes : (which + 1) * modes]
+
+    for half in range(2):
+        load(0, half).start()
+
+    arrived[:, rank:padded] = jnp.zeros((arrived.shape[0], padded - rank, arrived.shape[2]), jnp.float32)
+    barrier = pltpu.get_barrier_semaphore()
+    for peer in (x_peer, z_peer):
+        pl.semaphore_signal(
+            barrier, inc=1, device_id={"lon": peer}, device_id_type=pl.DeviceIdType.MESH
+        )
+
+    @pl.when(inner)
+    def _():
+        pl.semaphore_signal(
+            barrier, inc=1, device_id={"lon": m_peer}, device_id_type=pl.DeviceIdType.MESH
+        )
+
+    arrange(0)
+
+    @pl.when(inner)
+    def _():
+        pl.semaphore_wait(barrier, 3)
+
+    @pl.when(outer)
+    def _():
+        pl.semaphore_wait(barrier, 2)
+
+    @pl.when(outer)
+    def _():
+        for part in range(2):
+            samples_z(0, x, row, part).start()
+
+    for part in range(2):
+        samples_x(0, place, part).start()
 
     @pl.when(inner)
     def _():
         for copy in tables:
             copy.start()
 
-    arrived[:, rank:padded] = jnp.zeros((arrived.shape[0], padded - rank, arrived.shape[2]), jnp.float32)
-    barrier = pltpu.get_barrier_semaphore()
-    for peer in (x_peer, z_peer, m_peer):
-        pl.semaphore_signal(
-            barrier, inc=1, device_id={"lon": peer}, device_id_type=pl.DeviceIdType.MESH
-        )
-    pl.semaphore_wait(barrier, 3)
-
-    arrange(0)
-
-    @pl.when(outer)
-    def _():
-        samples_z(0, x, row).start()
+    for half in range(2):
+        load(1, half).start()
+
+    for t in range(1, AHEAD):
+        arrange(t)
+        for part in range(2):
+            samples_x(t, place, part).start()
 
     def step(i, carry):
-        @pl.when(outer & (i >= 2) & (i < chunks + 2))
+        @pl.when(outer & (i >= SENT_LAG) & (i < chunks + SENT_LAG))
         def _():
             for which in range(2):
-                samples_z(i - 2, which, row).wait_send()
-
-        @pl.when(i + 1 < chunks)
-        def _():
-            arrange(i + 1)
-
-        @pl.when(i < chunks)
-        def _():
-            samples_x(i, beside).wait_recv()
+                for part in range(2):
+                    samples_z(i - SENT_LAG, which, row, part).wait_send()
+
+        @pl.when(i + AHEAD < chunks)
+        def _():
+            arrange(i + AHEAD)
+            for part in range(2):
+                samples_x(i + AHEAD, place, part).start()
 
         @pl.when(outer & (i < chunks))
         def _():
-            samples_z(i, 1 - x, row).start()
+            for part in range(2):
+                samples_x(i, beside, part).wait_recv()
+                samples_z(i, 1 - x, row, part).start()
 
             @pl.when(i + 1 < chunks)
             def _():
-                samples_z(i + 1, x, row).start()
+                for part in range(2):
+                    samples_z(i + 1, x, row, part).start()
 
         @pl.when(outer & (i >= LAG) & (i < chunks + LAG))
         def _():
             t = i - LAG
-            modes_z(t, 1 - x, row).wait_recv()
-            modes_x(t).start()
-            modes_z(t, x, row).wait_recv()
+            for part in range(2):
+                modes_z(t, 1 - x, row, part).wait_recv()
+                modes_x(t, part).start()
+            for part in range(2):
+                modes_z(t, x, row, part).wait_recv()
             store(t, x, done.at[lax.rem(t, DONE_SLOTS), place])
 
         @pl.when(outer & (i >= LAG + 1) & (i < chunks + LAG + 1))
         def _():
             t = i - LAG - 1
-            modes_x(t).wait_send()
-            modes_x(t).wait_recv()
+            for part in range(2):
+                modes_x(t, part).wait_send()
+                modes_x(t, part).wait_recv()
             store(t, 1 - x, cross.at[lax.rem(t, CROSS_SLOTS)])
 
         @pl.when(inner & (i < chunks))
         def _():
-            for which in range(2):
-                samples_z(i, which, 1 - row).wait_recv()
+            for part in range(2):
+                samples_x(i, beside, part).wait_recv()
+                for which in range(2):
+                    samples_z(i, which, 1 - row, part).wait_recv()
 
             @pl.when(i == 0)
             def _():
@@ -385,47 +436,56 @@
         @pl.when(inner & (i >= 1) & (i < chunks + 1))
         def _():
             t = i - 1
-            code(t).wait_recv()
+            code(t, 0, 1 - row).wait_recv()
+            add_evens(t, 1 - row)
+            for which in (1 - x, x):
+                modes_z(t, which, 1 - row, 0).start()
+            code(t, 1, 1 - row).wait_recv()
+            add_evens(t, row)
+            modes_x(t, 0).start()
             decode(t)
-            modes_z(t, 1 - x, 1 - row).start()
-            modes_x(t).start()
-            modes_z(t, x, 1 - row).start()
+            modes_z(t, 1 - x, 1 - row, 1).start()
+            modes_x(t, 1).start()
+            modes_z(t, x, 1 - row, 1).start()
             store(t, x, done.at[lax.rem(t, DONE_SLOTS), place])
 
         @pl.when(inner & (i >= 2) & (i < chunks + 2))
         def _():
             t = i - 2
-            modes_x(t).wait_recv()
+            for part in range(2):
+                modes_x(t, part).wait_recv()
             store(t, 1 - x, cross.at[lax.rem(t, CROSS_SLOTS)])
 
         return carry
 
     lax.fori_loop(0, chunks + LAG + 1, step, 0)
 
-    for back in range(OTHER_SLOTS):
-        samples_x(chunks - 1 - back, place).wait_send()
+    for part in range(2):
+        for back in range(OTHER_SLOTS):
+            samples_x(chunks - 1 - back, place, part).wait_send()
 
     @pl.when(inner)
     def _():
-        for back in range(CODED_SLOTS):
-            code(chunks - 1 - back).wait_send()
-        for back in range(DONE_SLOTS):
-            for which in range(2):
-                modes_z(chunks - 1 - back, which, 1 - row).wait_send()
-            modes_x(chunks - 1 - back).wait_send()
+        for part in range(2):
+            for back in range(CODED_SLOTS):
+                code(chunks - 1 - back, part, row).wait_send()
+            for back in range(DONE_SLOTS):
+                for which in range(2):
+                    modes_z(chunks - 1 - back, which, 1 - row, part).wait_send()
+                modes_x(chunks - 1 - back, part).wait_send()
 
 
 def fused_local(state):
     points, fields, lat_dev = state.shape
     modes = points // 2
     groups = fields // SUBLANES
-    chunks = groups * PAIRS
+    chunks = groups * PIECES
     tables = all_tables(points)
     padded = tables[2].shape[1]
     rank = RADIX * points // 4 + EXTRA
     vmem = pl.BlockSpec(memory_space=pltpu.VMEM)
     hbm = pl.BlockSpec(memory_space=pl.ANY)
-    wide = 2 * LANES
+    wide = FIELDS * LANES
     dma = pltpu.SemaphoreType.DMA
 
     def f32(*shape):
@@ -454,16 +514,16 @@
             bf16(padded, wide),
             dma((2, 2)),
             dma((len(tables),)),
-            dma((OTHER_SLOTS,)),
-            dma((GRID_SLOTS,)),
+            dma((OTHER_SLOTS, 2)),
             dma((GRID_SLOTS, 2)),
-            dma((GRID_SLOTS, 2)),
-            dma((CODED_SLOTS,)),
-            dma((ARRIVED_SLOTS,)),
+            dma((GRID_SLOTS, 2, 2)),
+            dma((GRID_SLOTS, 2, 2)),
+            dma((CODED_SLOTS, 2)),
+            dma((ARRIVED_SLOTS, 2)),
+            dma((DONE_SLOTS, 2, 2)),
+            dma((DONE_SLOTS, 2, 2)),
             dma((DONE_SLOTS, 2)),
-            dma((DONE_SLOTS, 2)),
-            dma((DONE_SLOTS,)),
-            dma((CROSS_SLOTS,)),
+            dma((CROSS_SLOTS, 2)),
         ],
         compiler_params=pltpu.CompilerParams(
             collective_id=0, has_side_effects=True, vmem_limit_bytes=VMEM_LIMIT

time: 418 us -> 408 us (0.976)
  Pallas kernels: 412 us -> 402 us
    pallas_call x1, Pallas kernels: 412 us -> 402 us  [fused_local(): pl.pallas_call(functools.partial(kernel, chunks, rank), out_shape=pltpu.V...]
where the time goes in v2:
time: 408 us
  Pallas kernels  402 us (99%)
  local copies, waits for them, and re-layouts  6.16 us (2%)
    pallas_call x1, Pallas kernels, fused_local(): pl.pallas_call(functools.partial(kernel, chunks, rank), out_shape=pltpu.V...  402 us

profile of v2, /device:TPU:0, one launch (start us, length us, event | category | flops | bytes accessed | tf_op | source)
XLA Modules:
  0.0 408.2 jit_solution(1998187415414674438)
XLA Ops:
  0.0 402.1 %shard_map.73 = f32[2,128,8,2,8,128]{5,4,3,2,1,0:T(8,128)S(1)} custom-call(f32[256,64,256]{2,1,0:T(8,128)} %state.1, bf16[2,1024,1024]{2,1,0:T(8,128)(2,1)} %constant.12.clone.own_hi_all, bf16[2,1024,1024]{2,1,0:T(8,128)(2,1)} %constant.13.clone.own_lo_all, bf16[2,544,1024]{2,1,0:T(8,128)(2,1)} %constant.14.clone.sent_hi_all, ...), custom_call_target="tpu_custom_call" | custom-call | tf_op jit(solution)/shard_map/pallas_call | solution.py:497
  402.1 6.2 %copy.9 = f32[2,128,64,256]{3,2,1,0:T(8,128)} copy(f32[2,128,64,256]{3,2,1,0:T(8,128)S(1)} %bitcast.3) | data formatting | bytes 33554432

commit v3 on v2

--- a/solution.py
+++ b/solution.py
@@ -101,19 +101,17 @@
     power = (even * even).sum(1)
     spread = (odd @ even.T) * np.where(power > 1e-9, 1.0 / np.maximum(power, 1e-9), 0.0)
     left = odd - spread @ even
-    picked, columns = [], []
+    rest, basis = left, []
     for _ in range(EXTRA):
-        row, column = np.unravel_index(np.argmax(np.abs(left)), left.shape)
-        picked.append(row)
-        columns.append(left[:, column] / left[row, column])
-        left = left - np.outer(columns[-1], left[row])
-    columns = np.stack(columns, 1)
-    mix = np.linalg.solve(columns[picked].T, columns.T).T
+        row, column = np.unravel_index(np.argmax(np.abs(rest)), rest.shape)
+        basis.append(rest[row] / np.abs(rest[row]).max())
+        rest = rest - np.outer(rest[:, column] / rest[row, column], rest[row])
+    extra = np.linalg.qr(np.stack(basis, 1))[0].T
+    mix = left @ extra.T
     rank, padded = band + EXTRA, -(-(band + EXTRA) // 16) * 16
     sent = np.zeros((padded, count // 2))
-    sent[:rank] = np.concatenate([even[: band // 2], odd[picked], even[band // 2 :]])
+    sent[:rank] = np.concatenate([even[: band // 2], extra, even[band // 2 :]])
     fill = np.zeros((band, padded))
-    spread = spread - mix @ spread[picked]
     fill[:, :rank] = np.concatenate([spread[:, : band // 2], mix, spread[:, band // 2 :]], 1)
     return own, sent, fill
 

time: 408 us -> 408 us (level)
  no operation moved by 1% of the time
where the time goes in v3:
time: 408 us
  Pallas kernels  402 us (99%)
  local copies, waits for them, and re-layouts  6.16 us (2%)
    pallas_call x1, Pallas kernels, fused_local(): pl.pallas_call(functools.partial(kernel, chunks, rank), out_shape=pltpu.V...  402 us

profile of v3, /device:TPU:0, one launch (start us, length us, event | category | flops | bytes accessed | tf_op | source)
XLA Modules:
  0.0 408.2 jit_solution(6300338213480313277)
XLA Ops:
  0.0 402.1 %shard_map.73 = f32[2,128,8,2,8,128]{5,4,3,2,1,0:T(8,128)S(1)} custom-call(f32[256,64,256]{2,1,0:T(8,128)} %state.1, bf16[2,1024,1024]{2,1,0:T(8,128)(2,1)} %constant.12.clone.own_hi_all, bf16[2,1024,1024]{2,1,0:T(8,128)(2,1)} %constant.13.clone.own_lo_all, bf16[2,544,1024]{2,1,0:T(8,128)(2,1)} %constant.14.clone.sent_hi_all, ...), custom_call_target="tpu_custom_call" | custom-call | tf_op jit(solution)/shard_map/pallas_call | solution.py:495
  402.1 6.2 %copy.9 = f32[2,128,64,256]{3,2,1,0:T(8,128)} copy(f32[2,128,64,256]{3,2,1,0:T(8,128)S(1)} %bitcast.3) | data formatting | bytes 33554432

commit v4 on v3

--- a/solution.py
+++ b/solution.py
@@ -17,6 +17,7 @@
 FIELDS = 1
 PIECES = SUBLANES // FIELDS
 AHEAD = 2
+SLABS = 4
 SENT_LAG = 2
 EXTRA = 24
 LAG = 7
@@ -165,16 +166,19 @@
     def cut(part):
         return pl.ds(part * modes, modes)
 
+    def slab(part):
+        return pl.ds(part * (points // SLABS), points // SLABS)
+
     def samples_x(t, target_place, part):
         here, slot = lax.rem(t, OTHER_SLOTS), lax.rem(t, GRID_SLOTS)
         return remote(
-            other.at[here, cut(part)], grid.at[slot, target_place, cut(part)],
+            other.at[here, slab(part)], grid.at[slot, target_place, slab(part)],
             xs_send.at[here, part], xs_recv.at[slot, part], x_peer,
         )
 
     def samples_z(t, which, line, part):
         slot = lax.rem(t, GRID_SLOTS)
-        ref = grid.at[slot, line * 2 + which, cut(part)]
+        ref = grid.at[slot, line * 2 + which, slab(part)]
         return remote(ref, ref, zs_send.at[slot, which, part], zs_recv.at[slot, which, part], z_peer)
 
     def evens(line):
@@ -225,7 +229,7 @@
 
         @pl.when(t >= OTHER_SLOTS)
         def _():
-            for part in range(2):
+            for part in range(SLABS):
                 samples_x(t - OTHER_SLOTS, place, part).wait_send()
 
         slot, spare = lax.rem(t, GRID_SLOTS), lax.rem(t, OTHER_SLOTS)
@@ -355,10 +359,10 @@
 
     @pl.when(outer)
     def _():
-        for part in range(2):
+        for part in range(SLABS):
             samples_z(0, x, row, part).start()
 
-    for part in range(2):
+    for part in range(SLABS):
         samples_x(0, place, part).start()
 
     @pl.when(inner)
@@ -371,31 +375,31 @@
 
     for t in range(1, AHEAD):
         arrange(t)
-        for part in range(2):
+        for part in range(SLABS):
             samples_x(t, place, part).start()
 
     def step(i, carry):
         @pl.when(outer & (i >= SENT_LAG) & (i < chunks + SENT_LAG))
         def _():
             for which in range(2):
-                for part in range(2):
+                for part in range(SLABS):
                     samples_z(i - SENT_LAG, which, row, part).wait_send()
 
         @pl.when(i + AHEAD < chunks)
         def _():
             arrange(i + AHEAD)
-            for part in range(2):
+            for part in range(SLABS):
                 samples_x(i + AHEAD, place, part).start()
 
         @pl.when(outer & (i < chunks))
         def _():
-            for part in range(2):
+            for part in range(SLABS):
                 samples_x(i, beside, part).wait_recv()
                 samples_z(i, 1 - x, row, part).start()
 
             @pl.when(i + 1 < chunks)
             def _():
-                for part in range(2):
+                for part in range(SLABS):
                     samples_z(i + 1, x, row, part).start()
 
         @pl.when(outer & (i >= LAG) & (i < chunks + LAG))
@@ -418,7 +422,7 @@
 
         @pl.when(inner & (i < chunks))
         def _():
-            for part in range(2):
+            for part in range(SLABS):
                 samples_x(i, beside, part).wait_recv()
                 for which in range(2):
                     samples_z(i, which, 1 - row, part).wait_recv()
@@ -458,7 +462,7 @@
 
     lax.fori_loop(0, chunks + LAG + 1, step, 0)
 
-    for part in range(2):
+    for part in range(SLABS):
         for back in range(OTHER_SLOTS):
             samples_x(chunks - 1 - back, place, part).wait_send()
 
@@ -512,10 +516,10 @@
             bf16(padded, wide),
             dma((2, 2)),
             dma((len(tables),)),
-            dma((OTHER_SLOTS, 2)),
-            dma((GRID_SLOTS, 2)),
-            dma((GRID_SLOTS, 2, 2)),
-            dma((GRID_SLOTS, 2, 2)),
+            dma((OTHER_SLOTS, SLABS)),
+            dma((GRID_SLOTS, SLABS)),
+            dma((GRID_SLOTS, 2, SLABS)),
+            dma((GRID_SLOTS, 2, SLABS)),
             dma((CODED_SLOTS, 2)),
             dma((ARRIVED_SLOTS, 2)),
             dma((DONE_SLOTS, 2, 2)),

time: 408 us -> 409 us (level)
  no operation moved by 1% of the time
where the time goes in v4:
time: 409 us
  Pallas kernels  403 us (99%)
  local copies, waits for them, and re-layouts  6.16 us (2%)
    pallas_call x1, Pallas kernels, fused_local(): pl.pallas_call(functools.partial(kernel, chunks, rank), out_shape=pltpu.V...  403 us

profile of v4, /device:TPU:0, one launch (start us, length us, event | category | flops | bytes accessed | tf_op | source)
XLA Modules:
  0.0 408.8 jit_solution(7703751377495896118)
XLA Ops:
  0.0 402.6 %shard_map.73 = f32[2,128,8,2,8,128]{5,4,3,2,1,0:T(8,128)S(1)} custom-call(f32[256,64,256]{2,1,0:T(8,128)} %state.1, bf16[2,1024,1024]{2,1,0:T(8,128)(2,1)} %constant.12.clone.own_hi_all, bf16[2,1024,1024]{2,1,0:T(8,128)(2,1)} %constant.13.clone.own_lo_all, bf16[2,544,1024]{2,1,0:T(8,128)(2,1)} %constant.14.clone.sent_hi_all, ...), custom_call_target="tpu_custom_call" | custom-call | tf_op jit(solution)/shard_map/pallas_call | solution.py:499
  402.6 6.2 %copy.9 = f32[2,128,64,256]{3,2,1,0:T(8,128)} copy(f32[2,128,64,256]{3,2,1,0:T(8,128)S(1)} %bitcast.3) | data formatting | bytes 33554432
